TPU v7x, 32 devices: a whole 2x2x4 slice. The times are simulated.
32 devices in a mesh: dp: 2 (over x), kvh: 4 (over z), seq: 4 (over y, core).
Axes of the slice: x: 2, y: 2, z: 4, core: 2. Of those that a mesh axis runs over, the one named last changes fastest.
Arguments:
- x_hidden: bfloat16 [64, 12288], P('dp'), parts along dimension 0
- seq_lens: int32 [64], P('dp'), parts along dimension 0
- k_cache: bfloat16 [64, 2048, 8, 128], P('dp', 'seq', 'kvh'), parts along dimension 0
- v_cache: bfloat16 [64, 2048, 8, 128], P('dp', 'seq', 'kvh'), parts along dimension 0
- w_q: bfloat16 [12288, 96, 128], P(None, ('kvh', 'seq'))
- w_o: bfloat16 [96, 128, 12288], P(('kvh', 'seq'))
Outputs:
- output: bfloat16 [64, 12288], P('dp'), parts along dimension 0
There are 2 independent parts. A program takes and returns all parts, laid end to end along the dimension named above; an argument that names none is the same for every part.
All inputs are finite; a program needn't handle non-finite values.
Results may differ from a plain program's by a relative error of at most 0.0034335.
Values are sent between devices in bfloat16 or wider.
A program may use at most 1 GiB of HBM per device.

v0:
```python
import functools

import jax
import jax.numpy as jnp
import numpy as np
from jax import lax
from jax.experimental import pallas as pl
from jax.experimental.pallas import tpu as pltpu
from jax.sharding import PartitionSpec as P

ROPE_THETA = 500000.0
MESH = pl.DeviceIdType.MESH
F32 = jnp.float32
BF16 = jnp.bfloat16

ROWS = 32
DIM = 12288
HEADS = 6
HD = 128
SEQ = 4
KVH = 4
T_DEV = 512
TN = 2 * T_DEV
KC = 4
KD = DIM // KC
AHEAD = 7
VMEM_LIMIT = 60 * 2 ** 20
SLOTS = 8
BC = 8
NB = ROWS // BC
HALF = ROWS // 2
PITCH = 40
GROUP = 2
BLK = DIM // 8


def kernel(x_h, len_h, freq_h, k_h, v_h, wq_h, wo_h, out_ref,
           x_s, len_s, freq_s, wq_s, k_s, v_s, wo_s,
           posq, qg, q_t, ob, mlb, rb, attn_s, ypart, yrecv, yrecv2, zrecv,
           in_sem, wq_sem, k_sem, v_sem, wo_sem,
           qs_sem, qr_sem, cs_sem, cr_sem,
           ds_sem, dr_sem, ys_sem, yr_sem, zs_sem, zr_sem,
           azs_sem, azr_sem, ays_sem, ayr_sem, ads_sem, adr_sem, turn_sem):
    d = lax.axis_index('dp')
    z = lax.axis_index('kvh')
    me = lax.axis_index('seq')
    core = lax.rem(me, 2)
    y = lax.div(me, 2)

    def seq_peer(i):
        c = 1 - core if i & 1 else core
        yy = 1 - y if i & 2 else y
        return yy * 2 + c

    zs = [lax.rem(z + i, KVH) for i in (2, 1, 3, 0)]
    blocks = [zz * 2 + (1 - y) for zz in zs] + [zz * 2 + y for zz in zs]

    x_cp = pltpu.make_async_copy(x_h, x_s, in_sem.at[0])
    len_cp = pltpu.make_async_copy(len_h, len_s, in_sem.at[1])
    freq_cp = pltpu.make_async_copy(freq_h, freq_s, in_sem.at[2])
    len_cp.start()
    freq_cp.start()
    x_cp.start()

    def wq_cp(p, c):
        n = p * KC + c
        src = wq_h.at[pl.ds(2 * p, 2), pl.ds(c * KD, KD)]
        return pltpu.make_async_copy(src, wq_s.at[n % SLOTS], wq_sem.at[n])

    def k_cp(j):
        at = pl.ds(j * BC, BC)
        return pltpu.make_async_copy(k_h.at[at], k_s.at[at], k_sem.at[j])

    def v_cp(j):
        at = pl.ds(j * BC, BC)
        return pltpu.make_async_copy(v_h.at[at], v_s.at[at], v_sem.at[j])

    def wo_cp(i):
        src = wo_h.at[:, pl.ds(pl.multiple_of(blocks[i] * BLK, BLK), BLK)]
        return pltpu.make_async_copy(src, wo_s.at[i], wo_sem.at[i])

    fetches = [wq_cp(p, c) for p in range(3) for c in range(KC)]
    for j in range(NB):
        fetches += [k_cp(j), v_cp(j)]
    for cp in fetches[:AHEAD]:
        cp.start(priority=1)

    barrier = pltpu.get_barrier_semaphore()
    for i in range(1, SEQ):
        pl.semaphore_signal(barrier, inc=1, device_id=(d, z, seq_peer(i)), device_id_type=MESH)
    for i in range(1, KVH):
        pl.semaphore_signal(barrier, inc=1, device_id=(d, lax.rem(z + i, KVH), me), device_id_type=MESH)

    q_t[...] = jnp.zeros_like(q_t)
    lane = lax.broadcasted_iota(jnp.int32, (ROWS, TN), 1)
    row = lax.broadcasted_iota(jnp.int32, (ROWS, TN), 0)
    mine = (lane & 1) == (row >> 4)
    posq[...] = jnp.where(mine, me * T_DEV + (lane >> 1), 1 << 30)
    len_cp.wait()
    freq_cp.wait()
    rows128 = lax.broadcasted_iota(jnp.int32, (ROWS, HD), 0)
    lane128 = lax.broadcasted_iota(jnp.int32, (ROWS, HD), 1)
    pos = jnp.zeros((ROWS, HD), jnp.int32)
    for b in range(ROWS):
        pos = jnp.where(rows128 == b, len_s[b] - 1, pos)
    angle = pos.astype(F32) * freq_s[0:1, :]
    cosine = jnp.cos(angle)
    sine = jnp.sin(angle)
    sine = jnp.where(lane128 < HD // 2, -sine, sine)

    def q_copy(p, i, slot):
        at = (slot, pl.ds(2 * p, 2))
        return pltpu.make_async_remote_copy(
            src_ref=qg.at[at], dst_ref=qg.at[at],
            send_sem=qs_sem.at[p, i - 1], recv_sem=qr_sem.at[p, i - 1],
            device_id=(d, z, seq_peer(i)), device_id_type=MESH)

    x_cp.wait()
    for p in range(3):
        acc = [jnp.zeros((ROWS, HD), F32)] * 2
        for c in range(KC):
            n = p * KC + c
            wq_cp(p, c).wait()
            fetches[n + AHEAD].start(priority=1)
            at = slice(c * KD, (c + 1) * KD)
            for u in range(2):
                acc[u] = acc[u] + jnp.dot(x_s[:, at], wq_s[n % SLOTS, u], preferred_element_type=F32)
        for u in range(2):
            q = acc[u]
            q = q * cosine + pltpu.roll(q, HD // 2, axis=1) * sine
            qg[me, 2 * p + u] = q.astype(BF16)
        if p == 0:
            pl.semaphore_wait(barrier, SEQ - 1 + KVH - 1)
        for i in range(1, SEQ):
            q_copy(p, i, me).start()
    for cp in fetches[3 * KC + AHEAD:] + [wo_cp(0)]:
        cp.start(priority=1)
    for p in range(3):
        for i in range(1, SEQ):
            q_copy(p, i, seq_peer(i)).wait_recv()
    for i in range(1, 8):
        wo_cp(i).start(priority=1)
    q_rows = q_t.reshape(ROWS * PITCH, HD)
    for s in range(SEQ):
        for h in range(HEADS):
            q_rows[pl.ds(s * 8 + h, ROWS, stride=PITCH), :] = qg[s, h].astype(F32)

    ob_rows = ob.reshape(32 * ROWS, HD)
    ml_rows = mlb.reshape(ROWS * PITCH, HD)
    scale = HD ** -0.5

    def c_copy(j, i, dst, slot):
        at = pl.ds(j * BC, BC)
        return pltpu.make_async_remote_copy(
            src_ref=ob.at[at, dst], dst_ref=rb.at[slot, at],
            send_sem=cs_sem.at[j, i - 1], recv_sem=cr_sem.at[j, i - 1],
            device_id=(d, z, seq_peer(i)), device_id_type=MESH)

    lane8 = lax.broadcasted_iota(jnp.int32, (BC, HD), 1)
    lane32 = lax.broadcasted_iota(jnp.int32, (32, HD), 1)

    def piece(j, carry):
        k_cp(j).wait()
        v_cp(j).wait()
        for g in range(BC // 4):
            ws = []
            for h in range(2):
                b = j * BC + g * 4 + 2 * h
                qa, qb = q_t[b, :32].astype(BF16), q_t[b + 1, :32].astype(BF16)
                zero = jnp.zeros_like(qa)
                lhs = jnp.concatenate([jnp.concatenate([qa, zero], axis=1), jnp.concatenate([zero, qb], axis=1)], axis=0)
                rhs = jnp.concatenate([k_s[b], k_s[b + 1]], axis=1)
                both = lax.dot_general(lhs, rhs, (((1,), (1,)), ((), ())), preferred_element_type=F32)
                for u in range(2):
                    s = both[u * 32:(u + 1) * 32]
                    s = jnp.where(posq[...] < len_s[b + u], s * scale, -jnp.inf)
                    m = jnp.max(s, axis=1, keepdims=True)
                    w = jnp.exp(s - jnp.where(m == -jnp.inf, 0.0, m))
                    l = jnp.sum(w, axis=1, keepdims=True)
                    mlb[b + u, :32] = jnp.where(lane32 < 64, m, l)
                    ws.append(w.astype(BF16))
            b = j * BC + g * 4
            rhs = jnp.concatenate([v_s[b + u] for u in range(4)], axis=1)
            out = jnp.dot(jnp.concatenate(ws, axis=0), rhs, preferred_element_type=F32)
            for u in range(4):
                for v in range(SEQ):
                    ob[b + u, v] = out[u * 32 + v * 8:u * 32 + (v + 1) * 8, u * HD:(u + 1) * HD]
        for v in range(SEQ):
            stat = jnp.zeros((BC, HD), F32)
            for h in range(HEADS):
                of_head = ml_rows[pl.ds(j * BC * PITCH + v * 8 + h, BC, stride=PITCH), :]
                stat = jnp.where((lane8 & 63) == h, of_head, stat)
            ob_rows[pl.ds(j * BC * 32 + v * 8 + HEADS, BC, stride=32), :] = stat
        for i in range(1, SEQ):
            c_copy(j, i, seq_peer(i), me).start()
        return carry

    lax.fori_loop(0, NB, piece, 0)
    for p in range(3):
        for i in range(1, SEQ):
            q_copy(p, i, me).wait_send()
    def combine(half):
        for j in range(half * NB // 2, (half + 1) * NB // 2):
            for i in range(1, SEQ):
                c_copy(j, i, seq_peer(i), seq_peer(i)).wait_recv()
        at = pl.ds(half * HALF, HALF)
        rb_rows = rb.reshape(SEQ * ROWS * 8, HD)

        def part(i, h):
            if i == 0:
                return ob_rows[pl.ds(half * HALF * 32 + me * 8 + h, HALF, stride=32), :]
            return rb_rows[pl.ds((seq_peer(i) * ROWS + half * HALF) * 8 + h, HALF, stride=8), :]

        stats = [part(i, HEADS) for i in range(SEQ)]
        top = functools.reduce(jnp.maximum, stats)
        fac = [jnp.exp(st - top) for st in stats]
        total = functools.reduce(jnp.add, [f * pltpu.roll(st, 64, axis=1) for f, st in zip(fac, stats)])
        for h in range(HEADS):
            o = functools.reduce(jnp.add, [part(i, h) * f[:, h:h + 1] for i, f in enumerate(fac)])
            attn_s[at, h * HD:(h + 1) * HD] = (o / total[:, h:h + 1]).astype(BF16)

    def d_copy(half, n):
        return pltpu.make_async_remote_copy(
            src_ref=ypart.at[half, n], dst_ref=yrecv.at[n], send_sem=ds_sem.at[n], recv_sem=dr_sem.at[n],
            device_id=(d, z, seq_peer(1)), device_id_type=MESH)

    def y_copy(n):
        return pltpu.make_async_remote_copy(
            src_ref=ypart.at[core, n], dst_ref=yrecv2.at[n], send_sem=ys_sem.at[n], recv_sem=yr_sem.at[n],
            device_id=(d, z, seq_peer(2)), device_id_type=MESH)

    def z_copy(n, to, slot):
        return pltpu.make_async_remote_copy(
            src_ref=ypart.at[core, 4 + n], dst_ref=zrecv.at[slot], send_sem=zs_sem.at[n], recv_sem=zr_sem.at[slot],
            device_id=(d, to, me), device_id_type=MESH)

    def y_step(n):
        y_copy(n).wait_recv()
        ypart[core, 4 + n] = ypart[core, 4 + n] + yrecv2[n]
        if n < 3:
            z_copy(n, zs[n], z).start()

    def d_step(half, n):
        for u in range(n, n + GROUP):
            d_copy(half, u).wait_recv()
            ypart[half, u] = ypart[half, u] + yrecv[u]
            if u < 4:
                y_copy(u).start()

    for half in range(2):
        combine(half)
        for n in range(0, 8 + GROUP, GROUP):
            if n < 8:
                if half == 0:
                    for u in range(n, n + GROUP):
                        wo_cp(u).wait()
                for u in range(n, n + GROUP):
                    ypart[half, u] = jnp.dot(attn_s[half * HALF:(half + 1) * HALF, :], wo_s[u],
                                             preferred_element_type=F32)

                @pl.when(core != half)
                def _():
                    for u in range(n, n + GROUP):
                        d_copy(half, u).start()
            if 0 < n <= 4 or (n > 4 and half == 1):
                @pl.when(core == half)
                def _():
                    d_step(half, n - GROUP)
            if half == 1 and n in (2, 4):
                @pl.when(core == 0)
                def _():
                    d_step(0, n + 2)
            if half == 1 and n >= 4:
                @pl.when(core == 0)
                def _():
                    y_step((n - 4) // 2)

    @pl.when(core == 0)
    def _():
        y_step(3)

    @pl.when(core == 1)
    def _():
        for n in range(4):
            y_step(n)
        for n in range(3):
            z_copy(n, zs[n], z).wait_send()
        pl.semaphore_signal(turn_sem, inc=1, device_id=(d, z, seq_peer(1)), device_id_type=MESH)

    def block_at(half, block):
        return (pl.ds(pl.multiple_of(half * HALF, HALF), HALF), pl.ds(pl.multiple_of(block * BLK, BLK), BLK))

    def ag_z(i, block, to, frm):
        at = block_at(core, block)
        return pltpu.make_async_remote_copy(
            src_ref=out_ref.at[at], dst_ref=out_ref.at[at], send_sem=azs_sem.at[i], recv_sem=azr_sem.at[frm],
            device_id=(d, to, me), device_id_type=MESH)

    def ag_y(block, zz):
        at = block_at(core, block)
        return pltpu.make_async_remote_copy(
            src_ref=out_ref.at[at], dst_ref=out_ref.at[at], send_sem=ays_sem.at[zz], recv_sem=ayr_sem.at[zz],
            device_id=(d, z, seq_peer(2)), device_id_type=MESH)

    def ag_d(half, block):
        at = block_at(half, block)
        return pltpu.make_async_remote_copy(
            src_ref=out_ref.at[at], dst_ref=out_ref.at[at], send_sem=ads_sem.at[block], recv_sem=adr_sem.at[block],
            device_id=(d, z, seq_peer(1)), device_id_type=MESH)

    for n in range(3):
        z_copy(n, zs[n], zs[n]).wait_recv()
    own = z * 2 + y
    at = block_at(core, own)
    f = ypart[core, 7] + zrecv[zs[0]] + zrecv[zs[1]] + zrecv[zs[2]]
    out_ref[at] = (x_s[at].astype(F32) + f).astype(BF16)
    ag_d(core, own).start()

    @pl.when(core == 0)
    def _():
        pl.semaphore_wait(turn_sem, 1)

    for n in range(3):
        ag_z(n, own, zs[n], z).start()
    ag_y(own, z).start()
    for n in (1, 2, 0):
        b = zs[n] * 2 + y
        ag_z(n, b, zs[n], zs[n]).wait_recv()
        ag_y(b, zs[n]).start()
        ag_d(core, b).start()
    for zz in (z, zs[1], zs[2], zs[0]):
        b = zz * 2 + (1 - y)
        ag_y(b, zz).wait_recv()
        ag_d(core, b).start()
    for n in range(8):
        ag_d(1 - core, n).wait_recv()

    for j in range(NB):
        for i in range(1, SEQ):
            c_copy(j, i, seq_peer(i), me).wait_send()
    for n in range(8):
        d_copy(0, n).wait_send()
        ag_d(core, n).wait_send()
    for n in range(4):
        y_copy(n).wait_send()
        ag_y(n * 2 + y, n).wait_send()
    @pl.when(core == 0)
    def _():
        for n in range(3):
            z_copy(n, zs[n], z).wait_send()

    for n in range(3):
        ag_z(n, own, zs[n], z).wait_send()


def solution(mesh):
    half = HD // 2
    freq = ROPE_THETA ** (-np.arange(half, dtype=np.float64) * (2.0 / HD))
    freq = np.tile(np.concatenate([freq, freq]).astype(np.float32), (8, 1))
    dma = pltpu.SemaphoreType.DMA

    def local_step(x_hidden, seq_lens, k_loc, v_loc, wq_loc, wo_loc):
        any_spec = pl.BlockSpec(memory_space=pl.ANY)
        return pl.pallas_call(
            kernel,
            out_shape=pltpu.VMEM((ROWS, DIM), BF16),
            in_specs=[any_spec] * 7,
            out_specs=pl.BlockSpec(memory_space=pltpu.VMEM),
            scratch_shapes=[
                pltpu.VMEM((ROWS, DIM), BF16),
                pltpu.SMEM((ROWS,), jnp.int32),
                pltpu.VMEM((8, HD), F32),
                pltpu.VMEM((SLOTS, 2, KD, HD), BF16),
                pltpu.VMEM((ROWS, TN, HD), BF16),
                pltpu.VMEM((ROWS, TN, HD), BF16),
                pltpu.VMEM((8, HEADS * HD, BLK), BF16),
                pltpu.VMEM((ROWS, TN), jnp.int32),
                pltpu.VMEM((SEQ, HEADS, ROWS, HD), BF16),
                pltpu.VMEM((ROWS, PITCH, HD), F32),
                pltpu.VMEM((ROWS, SEQ, 8, HD), F32),
                pltpu.VMEM((ROWS, PITCH, HD), F32),
                pltpu.VMEM((SEQ, ROWS, 8, HD), F32),
                pltpu.VMEM((ROWS, HEADS * HD), BF16),
                pltpu.VMEM((2, 8, HALF, BLK), F32),
                pltpu.VMEM((8, HALF, BLK), F32),
                pltpu.VMEM((4, HALF, BLK), F32),
                pltpu.VMEM((4, HALF, BLK), F32),
                dma((3,)), dma((3 * KC,)), dma((NB,)), dma((NB,)), dma((8,)),
                dma((3, 3)), dma((3, 3)), dma((NB, 3)), dma((NB, 3)),
                dma((8,)), dma((8,)), dma((4,)), dma((4,)), dma((3,)), dma((4,)),
                dma((3,)), dma((4,)), dma((4,)), dma((4,)), dma((8,)), dma((8,)),
                pltpu.SemaphoreType.REGULAR,
            ],
            compiler_params=pltpu.CompilerParams(
                collective_id=0, has_side_effects=True, vmem_limit_bytes=VMEM_LIMIT),
            name='decode_step',
        )(x_hidden, seq_lens, jnp.asarray(freq),
          k_loc.reshape(ROWS, TN, HD), v_loc.reshape(ROWS, TN, HD),
          wq_loc.transpose(1, 0, 2), wo_loc.reshape(HEADS * HD, DIM))

    return jax.shard_map(
        local_step,
        mesh=mesh,
        in_specs=(P('dp', None), P('dp'), P('dp', 'seq', 'kvh', None), P('dp', 'seq', 'kvh', None),
                  P(None, ('kvh', 'seq'), None), P(('kvh', 'seq'), None, None)),
        out_specs=P('dp', None),
        check_vma=False)
```

profile of v0, /device:TPU:0, one launch (start us, length us, event | category | flops | bytes accessed | tf_op | source)
XLA Modules:
  0.0 48.6 jit_solution(16219562268058675928)
XLA Ops:
  0.0 47.8 %decode_step.1 = bf16[32,12288]{1,0:T(8,128)(2,1)S(1)} custom-call(bf16[32,12288]{1,0:T(8,128)(2,1)} %x_h.1, s32[32]{0:T(128)} %len_h.1, f32[8,128]{1,0:T(8,128)} %constant.2.clone.freq_h, bf16[32,1024,128]{2,1,0:T(8,128)(2,1)} %bitcast.6, bf16[32,1024,128]{2,1,0:T(8,128)(2,1)} %bitcast.7, bf16[6,12288,128]{2,1,0:T(8,128)(2,1)} %bitcast.4, ...), custom_call_target="tpu_custom_call" | custom-call | tf_op jit(solution)/shard_map/decode_step/pallas_call | solution.py:364
  47.8 0.9 %copy.9 = bf16[32,12288]{1,0:T(8,128)(2,1)} copy(bf16[32,12288]{1,0:T(8,128)(2,1)S(1)} %decode_step.1) | data formatting | bytes 1572864
where the time goes:
time: 48.8 us; the launch traced here: 48.6 us
  Pallas kernels  47.8 us (98%)
  local copies, waits for them, and re-layouts  0.88 us (2%)
    pallas_call x1, Pallas kernels, local_step(): pl.pallas_call(kernel, out_shape=pltpu.VMEM((ROWS, DIM), BF16), in_specs=...  47.8 us

commit v1 on v0

--- a/solution.py
+++ b/solution.py
@@ -52,7 +52,8 @@
         yy = 1 - y if i & 2 else y
         return yy * 2 + c
 
-    zs = [lax.rem(z + i, KVH) for i in (2, 1, 3, 0)]
+    far = 1 - lax.div(z, 2)
+    zs = [3 * far, 1 + far, z + 1 - 2 * lax.rem(z, 2), z]
     blocks = [zz * 2 + (1 - y) for zz in zs] + [zz * 2 + y for zz in zs]
 
     x_cp = pltpu.make_async_copy(x_h, x_s, in_sem.at[0])
@@ -179,12 +180,11 @@
                     l = jnp.sum(w, axis=1, keepdims=True)
                     mlb[b + u, :32] = jnp.where(lane32 < 64, m, l)
                     ws.append(w.astype(BF16))
-            b = j * BC + g * 4
-            rhs = jnp.concatenate([v_s[b + u] for u in range(4)], axis=1)
-            out = jnp.dot(jnp.concatenate(ws, axis=0), rhs, preferred_element_type=F32)
             for u in range(4):
+                b = j * BC + g * 4 + u
+                out = jnp.dot(ws[u], v_s[b], preferred_element_type=F32)
                 for v in range(SEQ):
-                    ob[b + u, v] = out[u * 32 + v * 8:u * 32 + (v + 1) * 8, u * HD:(u + 1) * HD]
+                    ob[b, v] = out[v * 8:(v + 1) * 8]
         for v in range(SEQ):
             stat = jnp.zeros((BC, HD), F32)
             for h in range(HEADS):
@@ -320,15 +320,16 @@
     def _():
         pl.semaphore_wait(turn_sem, 1)
 
+    az = [lax.rem(z + i, KVH) for i in (1, 3, 2)]
     for n in range(3):
-        ag_z(n, own, zs[n], z).start()
+        ag_z(n, own, az[n], z).start()
     ag_y(own, z).start()
-    for n in (1, 2, 0):
-        b = zs[n] * 2 + y
-        ag_z(n, b, zs[n], zs[n]).wait_recv()
-        ag_y(b, zs[n]).start()
+    for n in (0, 1, 2):
+        b = az[n] * 2 + y
+        ag_z(n, b, az[n], az[n]).wait_recv()
+        ag_y(b, az[n]).start()
         ag_d(core, b).start()
-    for zz in (z, zs[1], zs[2], zs[0]):
+    for zz in (z, az[0], az[1], az[2]):
         b = zz * 2 + (1 - y)
         ag_y(b, zz).wait_recv()
         ag_d(core, b).start()
@@ -350,7 +351,7 @@
             z_copy(n, zs[n], z).wait_send()
 
     for n in range(3):
-        ag_z(n, own, zs[n], z).wait_send()
+        ag_z(n, own, az[n], z).wait_send()
 
 
 def solution(mesh):

time: 48.8 us -> 47.3 us (0.969)
  Pallas kernels: 47.8 us -> 46.3 us
    pallas_call x1, Pallas kernels: 47.8 us -> 46.3 us  [local_step(): pl.pallas_call(kernel, out_shape=pltpu.VMEM((ROWS, DIM), BF16), in_specs=...]
where the time goes in v1:
time: 47.3 us; the launch traced here: 47.2 us
  Pallas kernels  46.3 us (98%)
  local copies, waits for them, and re-layouts  0.88 us (2%)
    pallas_call x1, Pallas kernels, local_step(): pl.pallas_call(kernel, out_shape=pltpu.VMEM((ROWS, DIM), BF16), in_specs=...  46.3 us

profile of v1, /device:TPU:0, one launch (start us, length us, event | category | flops | bytes accessed | tf_op | source)
XLA Modules:
  0.0 47.2 jit_solution(2654545465696091644)
XLA Ops:
  0.0 46.3 %decode_step.1 = bf16[32,12288]{1,0:T(8,128)(2,1)S(1)} custom-call(bf16[32,12288]{1,0:T(8,128)(2,1)} %x_h.1, s32[32]{0:T(128)} %len_h.1, f32[8,128]{1,0:T(8,128)} %constant.2.clone.freq_h, bf16[32,1024,128]{2,1,0:T(8,128)(2,1)} %bitcast.6, bf16[32,1024,128]{2,1,0:T(8,128)(2,1)} %bitcast.7, bf16[6,12288,128]{2,1,0:T(8,128)(2,1)} %bitcast.4, ...), custom_call_target="tpu_custom_call" | custom-call | tf_op jit(solution)/shard_map/decode_step/pallas_call | solution.py:365
  46.3 0.9 %copy.9 = bf16[32,12288]{1,0:T(8,128)(2,1)} copy(bf16[32,12288]{1,0:T(8,128)(2,1)S(1)} %decode_step.1) | data formatting | bytes 1572864

commit v2 on v1

--- a/solution.py
+++ b/solution.py
@@ -168,12 +168,8 @@
             for h in range(2):
                 b = j * BC + g * 4 + 2 * h
                 qa, qb = q_t[b, :32].astype(BF16), q_t[b + 1, :32].astype(BF16)
-                zero = jnp.zeros_like(qa)
-                lhs = jnp.concatenate([jnp.concatenate([qa, zero], axis=1), jnp.concatenate([zero, qb], axis=1)], axis=0)
-                rhs = jnp.concatenate([k_s[b], k_s[b + 1]], axis=1)
-                both = lax.dot_general(lhs, rhs, (((1,), (1,)), ((), ())), preferred_element_type=F32)
                 for u in range(2):
-                    s = both[u * 32:(u + 1) * 32]
+                    s = lax.dot_general(qa if u == 0 else qb, k_s[b + u], (((1,), (1,)), ((), ())), preferred_element_type=F32)
                     s = jnp.where(posq[...] < len_s[b + u], s * scale, -jnp.inf)
                     m = jnp.max(s, axis=1, keepdims=True)
                     w = jnp.exp(s - jnp.where(m == -jnp.inf, 0.0, m))
@@ -283,8 +279,6 @@
     def _():
         for n in range(4):
             y_step(n)
-        for n in range(3):
-            z_copy(n, zs[n], z).wait_send()
         pl.semaphore_signal(turn_sem, inc=1, device_id=(d, z, seq_peer(1)), device_id_type=MESH)
 
     def block_at(half, block):
@@ -345,10 +339,8 @@
     for n in range(4):
         y_copy(n).wait_send()
         ag_y(n * 2 + y, n).wait_send()
-    @pl.when(core == 0)
-    def _():
-        for n in range(3):
-            z_copy(n, zs[n], z).wait_send()
+    for n in range(3):
+        z_copy(n, zs[n], z).wait_send()
 
     for n in range(3):
         ag_z(n, own, az[n], z).wait_send()

time: 47.3 us -> 47.1 us (level)
  no operation moved by 1% of the time
where the time goes in v2:
time: 47.1 us; the launch traced here: 46.9 us
  Pallas kernels  46 us (98%)
  local copies, waits for them, and re-layouts  0.88 us (2%)
    pallas_call x1, Pallas kernels, local_step(): pl.pallas_call(kernel, out_shape=pltpu.VMEM((ROWS, DIM), BF16), in_specs=...  46 us

profile of v2, /device:TPU:0, one launch (start us, length us, event | category | flops | bytes accessed | tf_op | source)
XLA Modules:
  0.0 46.9 jit_solution(7510867516277441341)
XLA Ops:
  0.0 46.0 %decode_step.1 = bf16[32,12288]{1,0:T(8,128)(2,1)S(1)} custom-call(bf16[32,12288]{1,0:T(8,128)(2,1)} %x_h.1, s32[32]{0:T(128)} %len_h.1, f32[8,128]{1,0:T(8,128)} %constant.2.clone.freq_h, bf16[32,1024,128]{2,1,0:T(8,128)(2,1)} %bitcast.6, bf16[32,1024,128]{2,1,0:T(8,128)(2,1)} %bitcast.7, bf16[6,12288,128]{2,1,0:T(8,128)(2,1)} %bitcast.4, ...), custom_call_target="tpu_custom_call" | custom-call | tf_op jit(solution)/shard_map/decode_step/pallas_call | solution.py:357
  46.0 0.9 %copy.9 = bf16[32,12288]{1,0:T(8,128)(2,1)} copy(bf16[32,12288]{1,0:T(8,128)(2,1)S(1)} %decode_step.1) | data formatting | bytes 1572864

commit v3 on v2

--- a/solution.py
+++ b/solution.py
@@ -21,11 +21,11 @@
 KVH = 4
 T_DEV = 512
 TN = 2 * T_DEV
-KC = 4
+KC = 6
 KD = DIM // KC
-AHEAD = 7
+AHEAD = 10
 VMEM_LIMIT = 60 * 2 ** 20
-SLOTS = 8
+SLOTS = 12
 BC = 8
 NB = ROWS // BC
 HALF = ROWS // 2
@@ -122,7 +122,8 @@
         for c in range(KC):
             n = p * KC + c
             wq_cp(p, c).wait()
-            fetches[n + AHEAD].start(priority=1)
+            if n + AHEAD < len(fetches):
+                fetches[n + AHEAD].start(priority=1)
             at = slice(c * KD, (c + 1) * KD)
             for u in range(2):
                 acc[u] = acc[u] + jnp.dot(x_s[:, at], wq_s[n % SLOTS, u], preferred_element_type=F32)

time: 47.1 us -> 47 us (level)
  no operation moved by 1% of the time
where the time goes in v3:
time: 47 us; the launch traced here: 46.9 us
  Pallas kernels  46 us (98%)
  local copies, waits for them, and re-layouts  0.88 us (2%)
    pallas_call x1, Pallas kernels, local_step(): pl.pallas_call(kernel, out_shape=pltpu.VMEM((ROWS, DIM), BF16), in_specs=...  46 us

profile of v3, /device:TPU:0, one launch (start us, length us, event | category | flops | bytes accessed | tf_op | source)
XLA Modules:
  0.0 46.9 jit_solution(4470979466217608144)
XLA Ops:
  0.0 46.0 %decode_step.1 = bf16[32,12288]{1,0:T(8,128)(2,1)S(1)} custom-call(bf16[32,12288]{1,0:T(8,128)(2,1)} %x_h.1, s32[32]{0:T(128)} %len_h.1, f32[8,128]{1,0:T(8,128)} %constant.2.clone.freq_h, bf16[32,1024,128]{2,1,0:T(8,128)(2,1)} %bitcast.6, bf16[32,1024,128]{2,1,0:T(8,128)(2,1)} %bitcast.7, bf16[6,12288,128]{2,1,0:T(8,128)(2,1)} %bitcast.4, ...), custom_call_target="tpu_custom_call" | custom-call | tf_op jit(solution)/shard_map/decode_step/pallas_call | solution.py:358
  46.0 0.9 %copy.9 = bf16[32,12288]{1,0:T(8,128)(2,1)} copy(bf16[32,12288]{1,0:T(8,128)(2,1)S(1)} %decode_step.1) | data formatting | bytes 1572864
